TPU v7x, 32 devices: a whole 2x2x4 slice. The times are simulated.
32 devices in a mesh: gx: 2 (over x), gy: 4 (over y, core), gz: 4 (over z).
Axes of the slice: x: 2, y: 2, z: 4, core: 2. Of those that a mesh axis runs over, the one named last changes fastest.
Arguments:
- rhs: float32 [8, 8, 2, 16, 512], P(None, None, 'gx', 'gy', 'gz'), as said below
- blocks: bfloat16 [7, 8, 8, 2, 16, 512], P(None, None, None, 'gx', 'gy', 'gz'), as said below
Outputs:
- basis: float32 [4, 8, 8, 2, 16, 512], P(None, None, None, 'gx', 'gy', 'gz')
- hess: float32 [4, 8, 3, 8], replicated
Inputs may be any that keep to these rules, and one draw needn't show every extreme that they name: `rhs`: each cell's value is a random draw times a positive scale that varies smoothly over the grid. The operator couples each cell only to itself and its six face neighbours; its blocks are full and the block Krylov spaces keep full rank.
All inputs are finite; a program needn't handle non-finite values.
Results may differ from a plain program's by a relative error of at most 0.001.
Values sent between devices are 32-bit elements; how exact they have to be, the bound alone decides.
A program may use at most 64 MiB of HBM per device.

v0:
```python
import jax
import jax.numpy as jnp
from jax import lax
from jax.sharding import PartitionSpec as P

RHS = 8
ITERS = 3


HIGH = lax.Precision.HIGHEST


def with_halo(block, sides, width):
    for axis, dim in sides:
        count = lax.axis_size(axis)
        forward = [(i, i + 1) for i in range(count - 1)]
        backward = [(target, source) for source, target in forward]
        low = lax.ppermute(
            lax.slice_in_dim(block, block.shape[dim] - width, None, axis=dim), axis, forward
        )
        high = lax.ppermute(lax.slice_in_dim(block, 0, width, axis=dim), axis, backward)
        block = jnp.concatenate([low, block, high], axis=dim)
    return block


def couple(padded, blocks):
    views = [
        padded[:, :, 1:-1, 1:-1, 1:-1],
        padded[:, :, 2:, 1:-1, 1:-1],
        padded[:, :, :-2, 1:-1, 1:-1],
        padded[:, :, 1:-1, 2:, 1:-1],
        padded[:, :, 1:-1, :-2, 1:-1],
        padded[:, :, 1:-1, 1:-1, 2:],
        padded[:, :, 1:-1, 1:-1, :-2],
    ]
    total = jnp.zeros(views[0].shape, jnp.float32)
    for k in range(7):
        for j in range(views[0].shape[0]):
            column = blocks[k, :, j].astype(jnp.float32)
            total = total + column[:, None] * views[k][j][None]
    return total


def stencil(field, blocks):
    padded = with_halo(field, (("gx", 2), ("gy", 3), ("gz", 4)), 1)
    return couple(padded, blocks)


def pair(first, second):
    return jnp.einsum("arxyz,asxyz->rs", first, second, precision=HIGH)


def mix(field, matrix):
    return jnp.einsum("asxyz,sr->arxyz", field, matrix, precision=HIGH)


def normalizer(gram, eye):
    lower = jnp.linalg.cholesky(gram)
    inverse = lax.linalg.triangular_solve(lower, eye, left_side=True, lower=True)
    return (inverse.T, lower.T)


def shards(rhs, blocks):
    eye = jnp.eye(RHS, dtype=jnp.float32)
    hess = jnp.zeros((ITERS + 1, RHS, ITERS, RHS), jnp.float32)
    first_pair = None
    raw_image = stencil(rhs, blocks)
    gram_start, cross, square = lax.psum(
        (pair(rhs, rhs), pair(rhs, raw_image), pair(raw_image, raw_image)), ("gx", "gy", "gz")
    )
    scale, upper = normalizer(gram_start, eye)
    basis = [mix(rhs, scale)]
    images = [mix(raw_image, scale)]
    first_coeff = jnp.dot(jnp.dot(scale.T, cross, precision=HIGH), scale, precision=HIGH)
    first_gram = jnp.dot(jnp.dot(scale.T, square, precision=HIGH), scale, precision=HIGH)
    first_pair = (first_coeff, first_gram)
    for step in range(ITERS):
        image = images[step]
        if step == 0 and first_pair is not None:
            coeffs = [first_pair[0]]
            gram = first_pair[1]
        else:
            stacked = jnp.stack(basis + [image])
            partial_sums = jnp.einsum("karxyz,asxyz->krs", stacked, image, precision=HIGH)
            summed = lax.psum(partial_sums, ("gx", "gy", "gz"))
            coeffs = [summed[index] for index in range(len(basis))]
            gram = summed[len(basis)]
        rest = image
        for vector, coeff in zip(basis, coeffs):
            gram = gram - jnp.dot(coeff.T, coeff, precision=HIGH)
            rest = rest - mix(vector, coeff)
        scale, upper = normalizer(gram, eye)
        fresh = mix(rest, scale)
        basis.append(fresh)
        for index, coeff in enumerate(coeffs):
            hess = hess.at[index, :, step, :].set(coeff)
        hess = hess.at[step + 1, :, step, :].set(upper)
        if step + 1 < ITERS:
            images.append(stencil(fresh, blocks))
    return (jnp.stack(basis), hess)


def solution(mesh):
    placed = (P(None, None, "gx", "gy", "gz"), P(None, None, None, "gx", "gy", "gz"))
    return jax.shard_map(
        shards,
        mesh=mesh,
        in_specs=placed,
        out_specs=(P(None, None, None, "gx", "gy", "gz"), P()),
        check_vma=False,
    )
```

profile of v0, /device:TPU:0, one launch (start us, length us, event | category | flops | bytes accessed | tf_op | source)
XLA Modules:
  0.0 246.0 jit_solution(17078392354189909345)
XLA Ops:
  0.6 1.0 copy.203
  1.6 4.9 %collective-permute-start.1 = (f32[8,8,1,4,128]{4,1,3,2,0:T(8,128)S(1)}, f32[8,8,1,4,128]{4,1,3,2,0:T(8,128)S(1)}, u32[]{:S(2)}, u32[]{:S(2)}) collective-permute-start(f32[8,8,1,4,128]{4,1,3,2,0:T(8,128)S(1)} %copy.203), channel_id=1, source_target_pairs={{0,16},{1,17},{2,18},{3,19},{4,20},{5,21},{6,22},{7,23},{8,24},{9,... | collective-permute-start | bytes 393224 | tf_op jit(solution)/shard_map/ppermute | solution.py:18
  6.5 1.3 collective-permute-start
  7.8 0.9 bitcast_convert_fusion.53
  8.9 0.8 copy-done
  10.2 3.1 %collective-permute-done = f32[8,8,1,4,128]{4,1,3,2,0:T(8,128)S(1)} collective-permute-done((f32[8,8,1,4,128]{4,1,3,2,0:T(8,128)S(1)}, f32[8,8,1,4,128]{4,1,3,2,0:T(8,128)S(1)}, u32[]{:S(2)}, u32[]{:S(2)}) %collective-permute-start) | collective-permute-done | bytes 131104 | tf_op jit(solution)/shard_map/ppermute | solution.py:21
  13.4 1.3 collective-permute-start.2
  14.7 3.0 %collective-permute-start.3 = (f32[8,8,3,1,128]{4,1,3,2,0:T(8,128)S(1)}, f32[8,8,3,1,128]{4,1,3,2,0:T(8,128)S(1)}, u32[]{:S(2)}, u32[]{:S(2)}) collective-permute-start(f32[8,8,3,1,128]{4,1,3,2,0:T(8,128)S(1)} %get-tuple-element.285), channel_id=1, source_target_pairs={{0,4},{4,8},{8,12},{1,5},{5,9},{9,13},{2,6},{6,10},{10,14},{3,7},{... | collective-permute-start | bytes 294920 | tf_op jit(solution)/shard_map/ppermute | solution.py:18
  17.8 0.9 collective-permute-done.3
  18.9 0.9 copy.278
  19.8 3.5 %collective-permute-start.5 = (f32[8,8,3,6,1]{1,0,4,3,2:T(8,128)S(1)}, f32[8,8,3,6,1]{1,0,4,3,2:T(8,128)S(1)}, u32[]{:S(2)}, u32[]{:S(2)}) collective-permute-start(f32[8,8,3,6,1]{1,0,4,3,2:T(8,128)S(1)} %copy.278), channel_id=1, source_target_pairs={{0,1},{1,2},{2,3},{4,5},{5,6},{6,7},{8,9},{9,10},{10,11},{12,13},{... | collective-permute-start | bytes 13832 | tf_op jit(solution)/shard_map/ppermute | solution.py:18
  23.3 0.9 copy.277
  24.2 1.3 collective-permute-start.4
  25.6 0.9 copy.209
  26.7 4.0 %collective-permute-done.4 = f32[8,8,3,6,1]{1,0,4,3,2:T(8,128)S(1)} collective-permute-done((f32[8,8,3,6,1]{1,0,4,3,2:T(8,128)S(1)}, f32[8,8,3,6,1]{1,0,4,3,2:T(8,128)S(1)}, u32[]{:S(2)}, u32[]{:S(2)}) %collective-permute-start.4) | collective-permute-done | bytes 4640 | tf_op jit(solution)/shard_map/ppermute | solution.py:21
  30.7 0.9 copy.207
  31.8 1.0 multiply_add_fusion.2
  33.6 41.6 %all-reduce.1 = (f32[8,8]{0,1:T(8,128)S(1)}, f32[8,8]{1,0:T(8,128)S(1)}, f32[8,8]{0,1:T(8,128)S(1)}) all-reduce(f32[8,8]{0,1:T(8,128)S(1)} %convolution_bitcast_fusion.13, f32[8,8]{1,0:T(8,128)S(1)} %convolution_bitcast_fusion.12, f32[8,8]{0,1:T(8,128)S(1)} %convolution_bitcast_fusion.11), channel_id=1, replica_groups=mesh['gx'=2,'gy'=4,'gz'=4] {'gx','gy','gz'}, use_global_device_ids=true, to_apply=%region_0.0 | all-reduce | flops 192 | bytes 1536 | tf_op jit(solution)/shard_map/psum | solution.py:68
  75.3 0.7 cholesky.74
  76.7 0.6 fusion.488
  79.5 0.7 cholesky.85
  80.9 0.6 fusion.523
  83.0 1.3 collective-permute-start.6
  84.3 4.6 %collective-permute-start.7 = (f32[8,8,1,4,128]{4,1,3,0,2:T(8,128)S(1)}, f32[8,8,1,4,128]{4,1,3,0,2:T(8,128)S(1)}, u32[]{:S(2)}, u32[]{:S(2)}) collective-permute-start(f32[8,8,1,4,128]{4,1,3,0,2:T(8,128)S(1)} %bitcast.786), channel_id=1, source_target_pairs={{0,16},{1,17},{2,18},{3,19},{4,20},{5,21},{6,22},{7,23},{8,24},{9,... | collective-permute-start | bytes 393224 | tf_op jit(solution)/shard_map/ppermute | solution.py:18
  88.9 0.7 fusion.534
  90.1 0.7 copy-done.3
  90.8 2.8 %and_reduce_fusion = (pred[]{:T(512)}, pred[]{:T(512)}) fusion(s32[4]{0:T(128)S(1)} %copy-done.3, s32[1]{0:T(128)} %constant.288.clone.1, s32[1]{0:T(128)} %get-tuple-element.366, s32[1]{0:T(128)} %get-tuple-element.365, s32[1]{0:T(128)} %slice.1472, s32[1]{0:T(128)S(1)} %bitcast.825), kind=kLoop, calls=%fused_computation.849 | loop fusion | flops 54 | bytes 38 | tf_op jit(solution)/shard_map/reduce.18
  93.7 1.3 collective-permute-start.8
  95.0 3.0 %collective-permute-start.9 = (f32[8,8,3,1,128]{4,1,3,0,2:T(8,128)S(1)}, f32[8,8,3,1,128]{4,1,3,0,2:T(8,128)S(1)}, u32[]{:S(2)}, u32[]{:S(2)}) collective-permute-start(f32[8,8,3,1,128]{4,1,3,0,2:T(8,128)S(1)} %get-tuple-element.283), channel_id=1, source_target_pairs={{0,4},{4,8},{8,12},{1,5},{5,9},{9,13},{2,6},{6,10},{10,14},{3,7},{... | collective-permute-start | bytes 294920 | tf_op jit(solution)/shard_map/ppermute | solution.py:18
  98.0 0.9 collective-permute-done.9
  99.2 0.9 copy.218
  100.1 2.2 collective-permute-start.11
  102.3 0.9 copy.216
  103.2 1.3 collective-permute-start.10
  104.6 0.9 copy.219
  105.7 3.7 %collective-permute-done.10 = f32[8,8,3,6,1]{1,0,4,3,2:T(8,128)S(1)} collective-permute-done((f32[8,8,3,6,1]{1,0,4,3,2:T(8,128)S(1)}, f32[8,8,3,6,1]{1,0,4,3,2:T(8,128)S(1)}, u32[]{:S(2)}, u32[]{:S(2)}) %collective-permute-start.10) | collective-permute-done | bytes 4640 | tf_op jit(solution)/shard_map/ppermute | solution.py:21
  109.4 0.9 copy.217
  110.6 1.1 multiply_add_fusion.1
  111.7 1.6 convolution_bitcast_fusion.7
  113.3 42.8 %psum.38 = f32[3,8,8]{2,1,0:T(8,128)S(1)} all-reduce(f32[3,8,8]{2,1,0:T(8,128)S(1)} %convolution_bitcast_fusion.7), channel_id=1, replica_groups=mesh['gx'=2,'gy'=4,'gz'=4] {'gx','gy','gz'}, use_global_device_ids=true, to_apply=%region_5.8 | all-reduce | flops 192 | bytes 1536 | tf_op jit(solution)/shard_map/psum | solution.py:85
  157.0 0.7 cholesky.96
  158.4 0.6 fusion.524
  159.8 1.3 fusion.3
  161.4 1.3 collective-permute-start.12
  162.7 4.6 %collective-permute-start.13 = (f32[8,8,1,4,128]{4,1,3,0,2:T(8,128)S(1)}, f32[8,8,1,4,128]{4,1,3,0,2:T(8,128)S(1)}, u32[]{:S(2)}, u32[]{:S(2)}) collective-permute-start(f32[8,8,1,4,128]{4,1,3,0,2:T(8,128)S(1)} %bitcast.803), channel_id=1, source_target_pairs={{0,16},{1,17},{2,18},{3,19},{4,20},{5,21},{6,22},{7,23},{8,24},{9,... | collective-permute-start | bytes 393224 | tf_op jit(solution)/shard_map/ppermute | solution.py:18
  167.3 1.3 fusion.499
  168.7 1.1 collective-permute-done.13
  169.8 1.3 collective-permute-start.14
  171.1 3.0 %collective-permute-start.15 = (f32[8,8,3,1,128]{4,1,3,0,2:T(8,128)S(1)}, f32[8,8,3,1,128]{4,1,3,0,2:T(8,128)S(1)}, u32[]{:S(2)}, u32[]{:S(2)}) collective-permute-start(f32[8,8,3,1,128]{4,1,3,0,2:T(8,128)S(1)} %get-tuple-element.281), channel_id=1, source_target_pairs={{0,4},{4,8},{8,12},{1,5},{5,9},{9,13},{2,6},{6,10},{10,14},{3,7},{... | collective-permute-start | bytes 294920 | tf_op jit(solution)/shard_map/ppermute | solution.py:18
  174.1 0.9 collective-permute-done.15
  175.3 0.9 copy.230
  176.2 2.2 collective-permute-start.17
  178.4 0.9 copy.228
  179.3 1.3 collective-permute-start.16
  180.7 0.9 copy.231
  181.8 3.7 %collective-permute-done.16 = f32[8,8,3,6,1]{1,0,4,3,2:T(8,128)S(1)} collective-permute-done((f32[8,8,3,6,1]{1,0,4,3,2:T(8,128)S(1)}, f32[8,8,3,6,1]{1,0,4,3,2:T(8,128)S(1)}, u32[]{:S(2)}, u32[]{:S(2)}) %collective-permute-start.16) | collective-permute-done | bytes 4640 | tf_op jit(solution)/shard_map/ppermute | solution.py:21
  185.5 0.9 copy.229
  186.7 1.0 multiply_add_fusion
  187.8 1.6 convolution_bitcast_fusion.6
  189.4 44.9 %psum.39 = f32[4,8,8]{2,1,0:T(8,128)S(1)} all-reduce(f32[4,8,8]{2,1,0:T(8,128)S(1)} %convolution_bitcast_fusion.6), channel_id=1, replica_groups=mesh['gx'=2,'gy'=4,'gz'=4] {'gx','gy','gz'}, use_global_device_ids=true, to_apply=%region_6.9 | all-reduce | flops 256 | bytes 2048 | tf_op jit(solution)/shard_map/psum | solution.py:85
  235.7 0.7 cholesky.107
  238.6 1.1 fusion.7
  240.0 0.9 copy.245
  240.9 3.3 %fusion.498 = f32[4,8,3,8]{3,1,2,0:T(8,128)} fusion(f32[4,8,3,8]{3,1,2,0:T(8,128)} %copy-done.2, s32[]{:T(128)} %bitcast.379, s32[]{:T(128)} %bitcast.380, f32[4,8,8]{2,1,0:T(8,128)S(1)} %psum.39, pred[]{:T(512)} %get-tuple-element.118), kind=kLoop, calls=%fused_computation.797 | loop fusion | flops 64 | bytes 9984 | tf_op jit(solution)/shard_map/scatter | solution.py:96
  (133 shorter events, 17.8 us)
Async XLA Ops:
  0.6 8.1 %copy-start.1 = (bf16[7,8,8,1,4,128]{5,4,3,2,1,0:T(4,128)(2,1)S(1)}, bf16[7,8,8,1,4,128]{5,4,3,2,1,0:T(4,128)(2,1)}, u32[]{:S(2)}) copy-start(bf16[7,8,8,1,4,128]{5,4,3,2,1,0:T(4,128)(2,1)} %param.24) | copy-start | bytes 1376260
  1.6 8.5 %collective-permute-start.1 = (f32[8,8,1,4,128]{4,1,3,2,0:T(8,128)S(1)}, f32[8,8,1,4,128]{4,1,3,2,0:T(8,128)S(1)}, u32[]{:S(2)}, u32[]{:S(2)}) collective-permute-start(f32[8,8,1,4,128]{4,1,3,2,0:T(8,128)S(1)} %copy.203), channel_id=1, source_target_pairs={{0,16},{1,17},{2,18},{3,19},{4,20},{5,21},{6,22},{7,23},{8,24},{9,... | collective-permute-start | bytes 393224 | tf_op jit(solution)/shard_map/ppermute | solution.py:18
  6.5 6.9 %collective-permute-start = (f32[8,8,1,4,128]{4,1,3,2,0:T(8,128)S(1)}, f32[8,8,1,4,128]{4,1,3,2,0:T(8,128)S(1)}, u32[]{:S(2)}, u32[]{:S(2)}) collective-permute-start(f32[8,8,1,4,128]{4,1,3,2,0:T(8,128)S(1)} %copy.203), channel_id=1, source_target_pairs={{16,0},{17,1},{18,2},{19,3},{20,4},{21,5},{22,6},{23,7},{24,8},{25... | collective-permute-start | bytes 393224 | tf_op jit(solution)/shard_map/ppermute | solution.py:21
  8.8 0.9 copy-start
  13.4 4.4 %collective-permute-start.2 = (f32[8,8,3,1,128]{4,1,3,2,0:T(8,128)S(1)}, f32[8,8,3,1,128]{4,1,3,2,0:T(8,128)S(1)}, u32[]{:S(2)}, u32[]{:S(2)}) collective-permute-start(f32[8,8,3,1,128]{4,1,3,2,0:T(8,128)S(1)} %get-tuple-element.286), channel_id=1, source_target_pairs={{4,0},{8,4},{12,8},{5,1},{9,5},{13,9},{6,2},{10,6},{14,10},{7,3},{... | collective-permute-start | bytes 294920 | tf_op jit(solution)/shard_map/ppermute | solution.py:21
  14.7 4.0 %collective-permute-start.3 = (f32[8,8,3,1,128]{4,1,3,2,0:T(8,128)S(1)}, f32[8,8,3,1,128]{4,1,3,2,0:T(8,128)S(1)}, u32[]{:S(2)}, u32[]{:S(2)}) collective-permute-start(f32[8,8,3,1,128]{4,1,3,2,0:T(8,128)S(1)} %get-tuple-element.285), channel_id=1, source_target_pairs={{0,4},{4,8},{8,12},{1,5},{5,9},{9,13},{2,6},{6,10},{10,14},{3,7},{... | collective-permute-start | bytes 294920 | tf_op jit(solution)/shard_map/ppermute | solution.py:18
  19.8 5.7 %collective-permute-start.5 = (f32[8,8,3,6,1]{1,0,4,3,2:T(8,128)S(1)}, f32[8,8,3,6,1]{1,0,4,3,2:T(8,128)S(1)}, u32[]{:S(2)}, u32[]{:S(2)}) collective-permute-start(f32[8,8,3,6,1]{1,0,4,3,2:T(8,128)S(1)} %copy.278), channel_id=1, source_target_pairs={{0,1},{1,2},{2,3},{4,5},{5,6},{6,7},{8,9},{9,10},{10,11},{12,13},{... | collective-permute-start | bytes 13832 | tf_op jit(solution)/shard_map/ppermute | solution.py:18
  24.2 6.5 %collective-permute-start.4 = (f32[8,8,3,6,1]{1,0,4,3,2:T(8,128)S(1)}, f32[8,8,3,6,1]{1,0,4,3,2:T(8,128)S(1)}, u32[]{:S(2)}, u32[]{:S(2)}) collective-permute-start(f32[8,8,3,6,1]{1,0,4,3,2:T(8,128)S(1)} %copy.277), channel_id=1, source_target_pairs={{1,0},{2,1},{3,2},{5,4},{6,5},{7,6},{9,8},{10,9},{11,10},{13,12},{... | collective-permute-start | bytes 13832 | tf_op jit(solution)/shard_map/ppermute | solution.py:21
  83.0 10.6 %collective-permute-start.6 = (f32[8,8,1,4,128]{4,1,3,0,2:T(8,128)S(1)}, f32[8,8,1,4,128]{4,1,3,0,2:T(8,128)S(1)}, u32[]{:S(2)}, u32[]{:S(2)}) collective-permute-start(f32[8,8,1,4,128]{4,1,3,0,2:T(8,128)S(1)} %bitcast.785), channel_id=1, source_target_pairs={{16,0},{17,1},{18,2},{19,3},{20,4},{21,5},{22,6},{23,7},{24,8},{25... | collective-permute-start | bytes 393224 | tf_op jit(solution)/shard_map/ppermute | solution.py:21
  84.3 9.3 %collective-permute-start.7 = (f32[8,8,1,4,128]{4,1,3,0,2:T(8,128)S(1)}, f32[8,8,1,4,128]{4,1,3,0,2:T(8,128)S(1)}, u32[]{:S(2)}, u32[]{:S(2)}) collective-permute-start(f32[8,8,1,4,128]{4,1,3,0,2:T(8,128)S(1)} %bitcast.786), channel_id=1, source_target_pairs={{0,16},{1,17},{2,18},{3,19},{4,20},{5,21},{6,22},{7,23},{8,24},{9,... | collective-permute-start | bytes 393224 | tf_op jit(solution)/shard_map/ppermute | solution.py:18
  90.1 0.7 copy-start.3
  93.7 4.4 %collective-permute-start.8 = (f32[8,8,3,1,128]{4,1,3,0,2:T(8,128)S(1)}, f32[8,8,3,1,128]{4,1,3,0,2:T(8,128)S(1)}, u32[]{:S(2)}, u32[]{:S(2)}) collective-permute-start(f32[8,8,3,1,128]{4,1,3,0,2:T(8,128)S(1)} %get-tuple-element.284), channel_id=1, source_target_pairs={{4,0},{8,4},{12,8},{5,1},{9,5},{13,9},{6,2},{10,6},{14,10},{7,3},{... | collective-permute-start | bytes 294920 | tf_op jit(solution)/shard_map/ppermute | solution.py:21
  95.0 4.0 %collective-permute-start.9 = (f32[8,8,3,1,128]{4,1,3,0,2:T(8,128)S(1)}, f32[8,8,3,1,128]{4,1,3,0,2:T(8,128)S(1)}, u32[]{:S(2)}, u32[]{:S(2)}) collective-permute-start(f32[8,8,3,1,128]{4,1,3,0,2:T(8,128)S(1)} %get-tuple-element.283), channel_id=1, source_target_pairs={{0,4},{4,8},{8,12},{1,5},{5,9},{9,13},{2,6},{6,10},{10,14},{3,7},{... | collective-permute-start | bytes 294920 | tf_op jit(solution)/shard_map/ppermute | solution.py:18
  100.1 4.5 %collective-permute-start.11 = (f32[8,8,3,6,1]{1,0,4,3,2:T(8,128)S(1)}, f32[8,8,3,6,1]{1,0,4,3,2:T(8,128)S(1)}, u32[]{:S(2)}, u32[]{:S(2)}) collective-permute-start(f32[8,8,3,6,1]{1,0,4,3,2:T(8,128)S(1)} %copy.218), channel_id=1, source_target_pairs={{0,1},{1,2},{2,3},{4,5},{5,6},{6,7},{8,9},{9,10},{10,11},{12,13},{... | collective-permute-start | bytes 13832 | tf_op jit(solution)/shard_map/ppermute | solution.py:18
  103.2 6.2 %collective-permute-start.10 = (f32[8,8,3,6,1]{1,0,4,3,2:T(8,128)S(1)}, f32[8,8,3,6,1]{1,0,4,3,2:T(8,128)S(1)}, u32[]{:S(2)}, u32[]{:S(2)}) collective-permute-start(f32[8,8,3,6,1]{1,0,4,3,2:T(8,128)S(1)} %copy.216), channel_id=1, source_target_pairs={{1,0},{2,1},{3,2},{5,4},{6,5},{7,6},{9,8},{10,9},{11,10},{13,12},{... | collective-permute-start | bytes 13832 | tf_op jit(solution)/shard_map/ppermute | solution.py:21
  161.4 7.3 %collective-permute-start.12 = (f32[8,8,1,4,128]{4,1,3,0,2:T(8,128)S(1)}, f32[8,8,1,4,128]{4,1,3,0,2:T(8,128)S(1)}, u32[]{:S(2)}, u32[]{:S(2)}) collective-permute-start(f32[8,8,1,4,128]{4,1,3,0,2:T(8,128)S(1)} %bitcast.802), channel_id=1, source_target_pairs={{16,0},{17,1},{18,2},{19,3},{20,4},{21,5},{22,6},{23,7},{24,8},{25... | collective-permute-start | bytes 393224 | tf_op jit(solution)/shard_map/ppermute | solution.py:21
  162.7 7.1 %collective-permute-start.13 = (f32[8,8,1,4,128]{4,1,3,0,2:T(8,128)S(1)}, f32[8,8,1,4,128]{4,1,3,0,2:T(8,128)S(1)}, u32[]{:S(2)}, u32[]{:S(2)}) collective-permute-start(f32[8,8,1,4,128]{4,1,3,0,2:T(8,128)S(1)} %bitcast.803), channel_id=1, source_target_pairs={{0,16},{1,17},{2,18},{3,19},{4,20},{5,21},{6,22},{7,23},{8,24},{9,... | collective-permute-start | bytes 393224 | tf_op jit(solution)/shard_map/ppermute | solution.py:18
  169.8 4.4 %collective-permute-start.14 = (f32[8,8,3,1,128]{4,1,3,0,2:T(8,128)S(1)}, f32[8,8,3,1,128]{4,1,3,0,2:T(8,128)S(1)}, u32[]{:S(2)}, u32[]{:S(2)}) collective-permute-start(f32[8,8,3,1,128]{4,1,3,0,2:T(8,128)S(1)} %get-tuple-element.282), channel_id=1, source_target_pairs={{4,0},{8,4},{12,8},{5,1},{9,5},{13,9},{6,2},{10,6},{14,10},{7,3},{... | collective-permute-start | bytes 294920 | tf_op jit(solution)/shard_map/ppermute | solution.py:21
  171.1 4.0 %collective-permute-start.15 = (f32[8,8,3,1,128]{4,1,3,0,2:T(8,128)S(1)}, f32[8,8,3,1,128]{4,1,3,0,2:T(8,128)S(1)}, u32[]{:S(2)}, u32[]{:S(2)}) collective-permute-start(f32[8,8,3,1,128]{4,1,3,0,2:T(8,128)S(1)} %get-tuple-element.281), channel_id=1, source_target_pairs={{0,4},{4,8},{8,12},{1,5},{5,9},{9,13},{2,6},{6,10},{10,14},{3,7},{... | collective-permute-start | bytes 294920 | tf_op jit(solution)/shard_map/ppermute | solution.py:18
  174.1 0.9 copy-start.2
  176.2 4.5 %collective-permute-start.17 = (f32[8,8,3,6,1]{1,0,4,3,2:T(8,128)S(1)}, f32[8,8,3,6,1]{1,0,4,3,2:T(8,128)S(1)}, u32[]{:S(2)}, u32[]{:S(2)}) collective-permute-start(f32[8,8,3,6,1]{1,0,4,3,2:T(8,128)S(1)} %copy.230), channel_id=1, source_target_pairs={{0,1},{1,2},{2,3},{4,5},{5,6},{6,7},{8,9},{9,10},{10,11},{12,13},{... | collective-permute-start | bytes 13832 | tf_op jit(solution)/shard_map/ppermute | solution.py:18
  179.3 6.2 %collective-permute-start.16 = (f32[8,8,3,6,1]{1,0,4,3,2:T(8,128)S(1)}, f32[8,8,3,6,1]{1,0,4,3,2:T(8,128)S(1)}, u32[]{:S(2)}, u32[]{:S(2)}) collective-permute-start(f32[8,8,3,6,1]{1,0,4,3,2:T(8,128)S(1)} %copy.228), channel_id=1, source_target_pairs={{1,0},{2,1},{3,2},{5,4},{6,5},{7,6},{9,8},{10,9},{11,10},{13,12},{... | collective-permute-start | bytes 13832 | tf_op jit(solution)/shard_map/ppermute | solution.py:21
where the time goes:
time: 247 us; the launch traced here: 246 us
  blocking collectives  129 us (52%)
  starting transfers between devices  42.5 us (17%)
  other arithmetic  23.9 us (10%)
  local copies, waits for them, and re-layouts  18.8 us (8%)
  waiting for transfers between devices  18.3 us (7%)
  matrix products  11.8 us (5%)
    psum x2, blocking collectives, shards(): summed = lax.psum(partial_sums, ('gx', 'gy', 'gz'))  87.7 us
    psum x1, blocking collectives, shards(): lax.psum((pair(rhs, rhs), pair(rhs, raw_image), pair(raw_image, raw_image...  41.6 us
    ppermute x9, starting transfers between devices, with_halo(): lax.ppermute(lax.slice_in_dim(block, block.shape[dim] - width, None, axis...  30.9 us
    ppermute x9, waiting for transfers between devices, with_halo(): lax.ppermute(lax.slice_in_dim(block, 0, width, axis=dim), axis, backward)  14.6 us
    ppermute x9, starting transfers between devices, with_halo(): lax.ppermute(lax.slice_in_dim(block, 0, width, axis=dim), axis, backward)  11.6 us
    another operation x12, other arithmetic, normalizer(): lower = jnp.linalg.cholesky(gram)  5.63 us
    unnamed x14, local copies, waits for them, and re-layouts  5.27 us
    dot_general x11, matrix products, mix(): return jnp.einsum('asxyz,sr->arxyz', field, matrix, precision=HIGH)  4.97 us
  transfers between devices with their start and end apart: 18, of which 8 were waited for; matrix products, arithmetic and copies ran while one was open for 5% of the time, Pallas kernels for 0%

commit v1 on v0

v1 whole, which is shorter than its diff:
```python
import functools

import jax
import jax.numpy as jnp
from jax import lax
from jax.experimental import pallas as pl
from jax.experimental.pallas import tpu as pltpu
from jax.sharding import PartitionSpec as P

ITERS = 3
F32 = jnp.float32
HIGH = lax.Precision.HIGHEST
AXES = ("gx", "gy", "gz")


def dot_nt(a, b):
    return lax.dot_general(a, b, (((1,), (1,)), ((), ())), precision=HIGH, preferred_element_type=F32)


def dot_nn(a, b):
    return lax.dot_general(a, b, (((1,), (0,)), ((), ())), precision=HIGH, preferred_element_type=F32)


def kernel(
    mesh_sizes, nb, nr, ly, lz,
    rhs_hbm, blk_hbm, basis_hbm, hess_ref,
    rv, bv, vp, p1, p3, xb, zs, zr, ce, zp, ab, ob,
    x_send, x_recv, y_send, y_recv, z_send, z_recv, a_send, a_recv, in_sem, out_sem,
):
    nx, ny, nz = mesh_sizes
    ndev = nx * ny * nz
    gx, gy, gz = (lax.axis_index(a) for a in AXES)
    me = (gx * ny + gy) * nz + gz
    cells = ndev * ly * lz

    row = lax.broadcasted_iota(jnp.int32, (8, 128), 0)
    lane = lax.broadcasted_iota(jnp.int32, (8, 128), 1)

    in_rhs = pltpu.make_async_copy(rhs_hbm, rv, in_sem.at[0])
    in_blk = pltpu.make_async_copy(blk_hbm, bv, in_sem.at[1])
    in_rhs.start()
    in_blk.start()

    if nx == 1:
        x_sides = []
    elif nx == 2:
        x_sides = [(1 + gx, None, 1 - gx)]
    else:
        x_sides = [(1, gx < nx - 1, gx + 1), (2, gx > 0, gx - 1)]

    def when(cond, fn):
        if cond is None:
            fn()
        else:
            pl.when(cond)(fn)

    def remote(src, dst, ssem, rsem, dev):
        return pltpu.make_async_remote_copy(
            src_ref=src, dst_ref=dst, send_sem=ssem, recv_sem=rsem,
            device_id=dev, device_id_type=pl.DeviceIdType.MESH,
        )

    def x_copy(n, side, y):
        opposite = side if nx == 2 else 1 - side
        return remote(vp.at[n, 1 + y], xb.at[n, opposite, y], x_send.at[n, side, y],
                      x_recv.at[n, opposite, y], {"gx": x_sides[side][2]})

    def x_arrived(n, side, y):
        remote(vp.at[n, 1 + y], xb.at[n, side, y], x_send.at[n, side, y],
               x_recv.at[n, side, y], {"gx": x_sides[side][2]}).wait_recv()

    def y_copy(n, side):
        if side == 0:
            return remote(vp.at[n, ly], vp.at[n, 0], y_send.at[n, 0], y_recv.at[n, 0], {"gy": gy + 1})
        return remote(vp.at[n, 1], vp.at[n, ly + 1], y_send.at[n, 1], y_recv.at[n, 1], {"gy": gy - 1})

    def z_copy(n, side, y):
        target = gz - 1 if side == 0 else gz + 1
        return remote(zs.at[n, side, y], zr.at[n, side, y], z_send.at[n, side, y],
                      z_recv.at[n, side, y], {"gz": target})

    y_to = (gy < ny - 1, gy > 0)
    y_from = (gy > 0, gy < ny - 1)
    z_to = (gz > 0, gz < nz - 1)
    z_from = (gz < nz - 1, gz > 0)

    for side in range(2):
        @pl.when(jnp.logical_not(y_from[side]))
        def _():
            for n in range(ITERS):
                vp[n, 0 if side == 0 else ly + 1] = jnp.zeros((nb * 8, 128), F32)

        @pl.when(jnp.logical_not(z_from[side]))
        def _():
            for n in range(ITERS):
                zr[n, side] = jnp.zeros((ly, 8, 128), F32)

    if nx > 2:
        for side in range(2):
            @pl.when(jnp.logical_not(x_sides[side][1]))
            def _():
                for n in range(ITERS):
                    xb[n, side] = jnp.zeros((ly, nb * 8, 128), F32)

    def send_row(n, y):
        for side, entry in enumerate(x_sides):
            when(entry[1], lambda: x_copy(n, side, y).start())
        first = jnp.zeros((8, 128), F32)
        last = jnp.zeros((8, 128), F32)
        for a in range(nb):
            v = vp[n, 1 + y, a * 8:(a + 1) * 8]
            first = jnp.where(lane == a, pltpu.roll(v, a, 1) if a else v, first)
            last = jnp.where(lane == a, pltpu.roll(v, a + 1, 1), last)
        zs[n, 0, y] = first
        zs[n, 1, y] = last
        for side in range(2):
            pl.when(z_to[side])(lambda: z_copy(n, side, y).start())
        if y == ly - 1:
            pl.when(y_to[0])(lambda: y_copy(n, 0).start())
        if y == 0:
            pl.when(y_to[1])(lambda: y_copy(n, 1).start())

    order = [0] + ([ly - 1] if ly > 1 else []) + list(range(1, ly - 1))

    in_rhs.wait()
    for y in order:
        for a in range(nb):
            vp[0, 1 + y, a * 8:(a + 1) * 8] = rv[pl.ds(a * nr * ly + y, 8, stride=ly), :]
        send_row(0, y)

    in_blk.wait()
    terms = [0, 3, 4, 5, 6] + [e[0] for e in x_sides]
    total_abs = jnp.zeros((8, 128), F32)
    for t, k in enumerate(terms):
        def expand(i, carry):
            rows = bv[k, i].astype(F32)
            for j in range(nb):
                for y in range(ly):
                    r = j * ly + y
                    wide = jnp.broadcast_to(rows[r:r + 1], (8, 128))
                    ce[t, y, j, pl.ds(pl.multiple_of(i * 8, 8), 8), :] = wide
                    if j == 0 and y == 0:
                        pass
            return carry + jnp.sum(jnp.abs(rows), axis=0, keepdims=True)
        total_abs = lax.fori_loop(0, nb, expand, total_abs)
    trace = jnp.zeros((8, 128), F32)
    for y in range(ly):
        for i in range(nb):
            trace = trace + ce[0, y, i, i * 8:(i + 1) * 8]

    def wide(field):
        return jnp.concatenate(
            [field(y, a) for y in range(ly) for a in range(nb)], axis=1)

    def blockview(ref, n, off):
        if n is None:
            return lambda y, a: ref[y, a * 8:(a + 1) * 8]
        return lambda y, a: ref[n, off + y, a * 8:(a + 1) * 8]

    views = [blockview(vp, 0, 1), blockview(p1, None, 0), blockview(vp, 2, 1), blockview(p3, None, 0)]

    def stack(count):
        return jnp.concatenate([wide(v) for v in views[:count]], axis=0)

    def gram(n):
        d = dot_nt(wide(views[n]), stack(n + 1))
        w = 8 * (n + 1)
        rep_l = lax.broadcasted_iota(jnp.int32, (w, 128), 0)
        rep_m = lax.broadcasted_iota(jnp.int32, (w, 128), 1)
        return dot_nn(d, jnp.where(rep_m % 32 == rep_l, 1.0, 0.0).astype(F32))

    def peer(d):
        t = lax.rem(me + d, ndev)
        return (t // (ny * nz), (t // nz) % ny, t % nz)

    def ar_start(m, d8):
        packed = jnp.where(lane // 32 == row % 4, d8, 0.0)
        ab[m, me, 0:1] = jnp.sum(packed[0:4], axis=0, keepdims=True)
        ab[m, me, 1:2] = jnp.sum(packed[4:8], axis=0, keepdims=True)

        def body(d, c):
            remote(ab.at[m, me], ab.at[m, me], a_send.at[m], a_recv.at[m], peer(d)).start()
            return c
        lax.fori_loop(1, ndev, body, 0)

    def ar_done(m):
        pltpu.make_async_copy(ab.at[m, 0:ndev - 1], ab.at[m, 0:ndev - 1], a_recv.at[m]).wait()
        total = jnp.sum(ab[m], axis=0)
        z = jnp.where(row < 4, total[0:1], total[1:2])
        z = jnp.where(lane // 32 == row % 4, z, 0.0)
        z = z + pltpu.roll(z, 64, 1)
        return z + pltpu.roll(z, 32, 1)

    lane_sum = lambda x: jnp.sum(x, axis=1, keepdims=True)
    d0 = gram(0)
    d0 = d0 + jnp.where(lane % 32 == 8, lane_sum(trace), 0.0)
    d0 = d0 + jnp.where(lane % 32 == 9, lane_sum(total_abs), 0.0)
    ar_start(0, d0)

    def local_terms(n, y):
        pl_z = [z_from[0], z_from[1]]
        for side in range(2):
            pl.when(pl_z[side])(lambda: z_copy(n, side, y).wait_recv())
        if y == 0:
            pl.when(y_from[0])(lambda: y_copy(n, 0).wait_recv())
        if y == ly - 1:
            pl.when(y_from[1])(lambda: y_copy(n, 1).wait_recv())
        plus, minus = zr[n, 0, y], zr[n, 1, y]
        for j in range(nb):
            v = vp[n, 1 + y, j * 8:(j + 1) * 8]
            zp[0, j * 8:(j + 1) * 8] = jnp.where(
                lane == lz - 1, pltpu.roll(plus, lz - 1 - j, 1), pltpu.roll(v, lz - 1, 1))
            zp[1, j * 8:(j + 1) * 8] = jnp.where(
                lane == 0, pltpu.roll(minus, lz - j, 1) if j else minus, pltpu.roll(v, 1, 1))

        def body(j, acc):
            at = pl.ds(pl.multiple_of(j * 8, 8), 8)
            values = [vp[n, 1 + y, at, :], vp[n, 2 + y, at, :], vp[n, y, at, :], zp[0, at, :], zp[1, at, :]]
            for t, v in enumerate(values):
                acc = acc + ce[t, y, j].reshape(nb, 8, 128) * v[None]
            return acc
        return lax.fori_loop(0, nb, body, jnp.zeros((nb, 8, 128), F32))

    def x_terms(n, y, acc):
        for side, entry in enumerate(x_sides):
            when(entry[1], lambda: x_arrived(n, side, y))

            def body(j, acc):
                at = pl.ds(pl.multiple_of(j * 8, 8), 8)
                return acc + ce[5 + side, y, j].reshape(nb, 8, 128) * xb[n, side, y, at, :][None]
            acc = lax.fori_loop(0, nb, body, acc)
        return acc.reshape(nb * 8, 128)

    for y in order:
        vp[1, 1 + y] = x_terms(0, y, local_terms(0, y))
        send_row(1, y)
    red0 = ar_done(0)
    sigma = jnp.broadcast_to(red0[0:1, 8:9] / (8.0 * cells), (8, 128))
    nu = jnp.broadcast_to(red0[0:1, 9:10] / (8.0 * cells), (8, 128))
    inv = 1.0 / nu
    sig1, inv1 = sigma[0:1], inv[0:1]
    for y in range(ly):
        p1[y] = (vp[1, 1 + y] - sig1 * vp[0, 1 + y]) * inv1
    ar_start(1, gram(1))

    for y in order:
        image = x_terms(1, y, local_terms(1, y))
        vp[2, 1 + y] = ((image - sig1 * vp[1, 1 + y]) * inv1 - sig1 * p1[y]) * inv1
        send_row(2, y)
    ar_start(2, gram(2))

    for y in order:
        image = x_terms(2, y, local_terms(2, y))
        p3[y] = (image - sig1 * vp[2, 1 + y]) * inv1
    ar_start(3, gram(3))

    weights, factors = [], []
    empty = jnp.zeros((8, 128), F32)

    def pad_rows(pieces):
        return jnp.concatenate(pieces + [empty] * (16 - len(pieces)), axis=0)

    def factor(n, red):
        base = 8 * n
        unit = jnp.where(lane == base + row, 1.0, 0.0).astype(F32)
        d = jnp.where(lane < base + 8, red, 0.0)
        shifted = pltpu.roll(d, 128 - base, 1) if n else d
        if n:
            rt = dot_nt(d, pad_rows(weights))
            s = shifted - dot_nt(rt, pad_rows([rt]))
            aug = unit - rt
        else:
            rt = empty
            s = shifted
            aug = unit
        cols = [jnp.broadcast_to(s[:, c:c + 1], (8, 128)) for c in range(8)]
        low = rt
        for k in range(8):
            piv = jnp.broadcast_to(cols[k][k:k + 1], (8, 128))
            rs = lax.rsqrt(piv)
            rs = rs * (1.5 - 0.5 * piv * rs * rs)
            lk = jnp.where(row >= k, cols[k] * rs, 0.0)
            low = low + jnp.where(lane == base + k, lk, 0.0)
            arow = jnp.broadcast_to(aug[k:k + 1], (8, 128)) * rs
            aug = jnp.where(row == k, arow, aug - jnp.where(row > k, lk, 0.0) * arow)
            for c in range(k + 1, 8):
                cols[c] = cols[c] - lk * jnp.broadcast_to(lk[c:c + 1], (8, 128))
        weights.append(dot_nn(aug, pad_rows(weights + [unit])) if n else aug)
        factors.append(low)

    def emit(n):
        q = dot_nn(weights[n][:, :8 * (n + 1)], stack(n + 1))
        for y in range(ly):
            for a in range(nb):
                c = (y * nb + a) * 128
                ob[n, pl.ds(a * nr * ly + y, 8, stride=ly), :] = q[:, c:c + 128]
        pltpu.make_async_copy(ob.at[n], basis_hbm.at[n], out_sem.at[n]).start()

    factor(0, red0)
    emit(0)
    factor(1, ar_done(1))
    emit(1)
    factor(2, ar_done(2))
    emit(2)
    factor(3, ar_done(3))
    emit(3)
    h = dot_nn(jnp.concatenate(weights[:3] + [empty], axis=0), pad_rows(factors[1:]))
    hr = lax.broadcasted_iota(jnp.int32, (32, 128), 0)
    hl = lax.broadcasted_iota(jnp.int32, (32, 128), 1)
    hess_ref[...] = h * nu[0:1] + jnp.where(hr == hl, sigma[0:1], 0.0)

    for n in range(ITERS):
        for y in range(ly):
            for side, entry in enumerate(x_sides):
                when(entry[1], lambda: x_copy(n, side, y).wait_send())
            for side in range(2):
                pl.when(z_to[side])(lambda: z_copy(n, side, y).wait_send())
        for side in range(2):
            pl.when(y_to[side])(lambda: y_copy(n, side).wait_send())
    for m in range(4):
        pltpu.make_async_copy(ab.at[m, 0:ndev - 1], ab.at[m, 0:ndev - 1], a_send.at[m]).wait()
        pltpu.make_async_copy(ob.at[m], basis_hbm.at[m], out_sem.at[m]).wait()


def shards(mesh_sizes, rhs, blocks):
    nb, nr, lx, ly, lz = rhs.shape
    assert nb == 8 and nr == 8 and lx == 1 and lz == 128
    nx, ny, nz = mesh_sizes
    ndev = nx * ny * nz
    sides = max(1, min(2, nx - 1))
    rhs2 = rhs.reshape(nb * nr * ly, lz)
    blk2 = blocks.reshape(7, nb, nb * ly, lz)
    dma = pltpu.SemaphoreType.DMA
    vm = lambda *s: pltpu.VMEM(s, F32)
    basis, hess = pl.pallas_call(
        functools.partial(kernel, mesh_sizes, nb, nr, ly, lz),
        out_shape=(
            jax.ShapeDtypeStruct((ITERS + 1, nb * nr * ly, lz), F32),
            jax.ShapeDtypeStruct((32, 128), F32),
        ),
        in_specs=[pl.BlockSpec(memory_space=pl.ANY)] * 2,
        out_specs=(pl.BlockSpec(memory_space=pl.ANY), pl.BlockSpec(memory_space=pltpu.VMEM)),
        scratch_shapes=[
            vm(nb * nr * ly, lz),
            pltpu.VMEM((7, nb, nb * ly, lz), jnp.bfloat16),
            vm(ITERS, ly + 2, nb * 8, lz),
            vm(ly, nb * 8, lz),
            vm(ly, nb * 8, lz),
            vm(ITERS, sides, ly, nb * 8, lz),
            vm(ITERS, 2, ly, 8, lz),
            vm(ITERS, 2, ly, 8, lz),
            vm(5 + sides, ly, nb, nb * 8, lz),
            vm(2, nb * 8, lz),
            vm(ITERS + 1, ndev, 2, lz),
            vm(ITERS + 1, nb * nr * ly, lz),
            dma((ITERS, sides, ly)), dma((ITERS, sides, ly)),
            dma((ITERS, 2)), dma((ITERS, 2)),
            dma((ITERS, 2, ly)), dma((ITERS, 2, ly)),
            dma((ITERS + 1,)), dma((ITERS + 1,)),
            dma((2,)), dma((ITERS + 1,)),
        ],
        compiler_params=pltpu.CompilerParams(has_side_effects=True, vmem_limit_bytes=48 * 1024 * 1024),
    )(rhs2, blk2)
    basis = basis.reshape(ITERS + 1, nb, nr, lx, ly, lz)
    hess = hess[:24, :32].reshape(3, 8, 4, 8).transpose(2, 3, 0, 1)
    return basis, hess


def solution(mesh):
    sizes = tuple(mesh.shape[a] for a in AXES)
    return jax.shard_map(
        functools.partial(shards, sizes),
        mesh=mesh,
        in_specs=(P(None, None, "gx", "gy", "gz"), P(None, None, None, "gx", "gy", "gz")),
        out_specs=(P(None, None, None, "gx", "gy", "gz"), P()),
        check_vma=False,
    )
```

time: 247 us -> 36.5 us (0.15)
  blocking collectives: 129 us -> 0 us
  starting transfers between devices: 42.5 us -> 0 us
  Pallas kernels: 0 us -> 32.1 us
  other arithmetic: 23.9 us -> 0 us
  waiting for transfers between devices: 18.3 us -> 0 us
  local copies, waits for them, and re-layouts: 18.8 us -> 3.5 us
  matrix products: 11.8 us -> 0 us
    psum x3 -> x0, blocking collectives: 129 us -> none  [the longest x2 87.7 us: shards(): summed = lax.psum(partial_sums, ('gx', 'gy', 'gz'))]
    ppermute x18 -> x0, starting transfers between devices: 42.5 us -> none  [the longest x9 30.9 us: with_halo(): lax.ppermute(lax.slice_in_dim(block, block.shape[dim] - width, None, axis...]
    pallas_call x0 -> x1, Pallas kernels: none -> 32.1 us  [shards(): pl.pallas_call(functools.partial(kernel, mesh_sizes, nb, nr, ly, lz), out...]
    ppermute x18 -> x0, waiting for transfers between devices: 18.3 us -> none  [the longest x9 14.6 us: with_halo(): lax.ppermute(lax.slice_in_dim(block, 0, width, axis=dim), axis, backward)]
    another operation x23 -> x0, other arithmetic: 13.5 us -> none  [the longest x12 5.63 us: normalizer(): lower = jnp.linalg.cholesky(gram)]
    dot_general x26 -> x0, matrix products: 11 us -> none  [the longest x11 4.97 us: mix(): return jnp.einsum('asxyz,sr->arxyz', field, matrix, precision=HIGH)]
    ppermute x6 -> x0, local copies, waits for them, and re-layouts: 5.45 us -> none  [the longest x3 2.73 us: with_halo(): lax.ppermute(lax.slice_in_dim(block, block.shape[dim] - width, None, axis...]
    scatter x2 -> x0, other arithmetic: 4.57 us -> none  [shards(): hess = hess.at[index, :, step, :].set(coeff)]
  transfers between devices with their start and end apart: 18 -> 0, of which waited for: 8 -> 0; matrix products, arithmetic and copies ran while one was open for 5% -> 0% of each run, Pallas kernels for 0% -> 0%
where the time goes in v1:
time: 36.5 us; the launch traced here: 36.3 us
  Pallas kernels  32.1 us (88%)
  local copies, waits for them, and re-layouts  3.5 us (10%)
  between operations  0.66 us (2%)
    pallas_call x1, Pallas kernels, shards(): pl.pallas_call(functools.partial(kernel, mesh_sizes, nb, nr, ly, lz), out...  32.1 us
    unnamed x5, local copies, waits for them, and re-layouts  2.71 us
    reshape x2, local copies, waits for them, and re-layouts, shards(): hess = hess[:24, :32].reshape(3, 8, 4, 8).transpose(2, 3, 0, 1)  0.79 us

profile of v1, /device:TPU:0, one launch (start us, length us, event | category | flops | bytes accessed | tf_op | source)
XLA Modules:
  0.0 36.3 jit_solution(16284784428025881029)
XLA Ops:
  0.6 0.0 copy-start
  0.6 1.0 %copy-done = bf16[7,8,8,1,4,128]{5,4,3,2,1,0:T(4,128)(2,1)S(1)} copy-done((bf16[7,8,8,1,4,128]{5,4,3,2,1,0:T(4,128)(2,1)S(1)}, bf16[7,8,8,1,4,128]{5,4,3,2,1,0:T(4,128)(2,1)}, u32[]{:S(2)}) %copy-start) | copy-done | bytes 458776
  1.6 0.0 copy-start.1
  1.7 0.9 %copy-done.1 = f32[8,8,1,4,128]{4,3,2,1,0:T(4,128)S(1)} copy-done((f32[8,8,1,4,128]{4,3,2,1,0:T(4,128)S(1)}, f32[8,8,1,4,128]{4,3,2,1,0:T(4,128)}, u32[]{:S(2)}) %copy-start.1) | copy-done | bytes 131096
  2.6 32.1 %shard_map.41 = (f32[4,256,128]{2,1,0:T(8,128)S(1)}, f32[32,128]{1,0:T(8,128)S(1)}) custom-call(f32[256,128]{1,0:T(8,128)S(1)} %bitcast.8, bf16[7,8,32,128]{3,2,1,0:T(8,128)(2,1)S(1)} %bitcast.7), custom_call_target="tpu_custom_call" | custom-call | tf_op jit(solution)/shard_map/pallas_call | solution.py:335
  34.7 0.1 reshape.19
  34.8 0.7 %copy.4 = f32[3,8,4,8]{1,3,0,2:T(8,128)} copy(f32[3,8,4,8]{3,2,1,0:T(4,128)S(1)} %reshape.19) | data formatting | bytes 6144 | tf_op jit(solution)/shard_map/reshape | solution.py:365
  35.5 0.8 %copy.7 = f32[4,8,8,1,4,128]{5,4,3,2,1,0:T(4,128)} copy(f32[4,8,8,1,4,128]{5,4,3,2,1,0:T(4,128)S(1)} %bitcast.6) | data formatting | bytes 1048576
  (1 shorter events, 0.0 us)
Async XLA Ops:
  0.6 1.0 %copy-start = (bf16[7,8,8,1,4,128]{5,4,3,2,1,0:T(4,128)(2,1)S(1)}, bf16[7,8,8,1,4,128]{5,4,3,2,1,0:T(4,128)(2,1)}, u32[]{:S(2)}) copy-start(bf16[7,8,8,1,4,128]{5,4,3,2,1,0:T(4,128)(2,1)} %param.3) | copy-start | bytes 1376260
  1.6 0.9 %copy-start.1 = (f32[8,8,1,4,128]{4,3,2,1,0:T(4,128)S(1)}, f32[8,8,1,4,128]{4,3,2,1,0:T(4,128)}, u32[]{:S(2)}) copy-start(f32[8,8,1,4,128]{4,3,2,1,0:T(4,128)} %param.2) | copy-start | bytes 393220

commit v2 on v1

--- a/solution.py
+++ b/solution.py
@@ -36,10 +36,21 @@
     row = lax.broadcasted_iota(jnp.int32, (8, 128), 0)
     lane = lax.broadcasted_iota(jnp.int32, (8, 128), 1)
 
+    def peer(d):
+        t = lax.rem(me + d, ndev)
+        return (t // (ny * nz), (t // nz) % ny, t % nz)
+
+    barrier = pltpu.get_barrier_semaphore()
+
+    def greet(d, c):
+        pl.semaphore_signal(barrier, inc=1, device_id=peer(d), device_id_type=pl.DeviceIdType.MESH)
+        return c
+
     in_rhs = pltpu.make_async_copy(rhs_hbm, rv, in_sem.at[0])
     in_blk = pltpu.make_async_copy(blk_hbm, bv, in_sem.at[1])
     in_rhs.start()
     in_blk.start()
+    lax.fori_loop(1, ndev, greet, 0)
 
     if nx == 1:
         x_sides = []
@@ -126,6 +137,8 @@
     for y in order:
         for a in range(nb):
             vp[0, 1 + y, a * 8:(a + 1) * 8] = rv[pl.ds(a * nr * ly + y, 8, stride=ly), :]
+    pl.semaphore_wait(barrier, ndev - 1)
+    for y in order:
         send_row(0, y)
 
     in_blk.wait()
@@ -152,26 +165,45 @@
         return jnp.concatenate(
             [field(y, a) for y in range(ly) for a in range(nb)], axis=1)
 
+    def eight(a):
+        return a * 8 if isinstance(a, int) else pl.multiple_of(a * 8, 8)
+
     def blockview(ref, n, off):
         if n is None:
-            return lambda y, a: ref[y, a * 8:(a + 1) * 8]
-        return lambda y, a: ref[n, off + y, a * 8:(a + 1) * 8]
+            return lambda y, a: ref[y, pl.ds(eight(a), 8), :]
+        return lambda y, a: ref[n, off + y, pl.ds(eight(a), 8), :]
 
     views = [blockview(vp, 0, 1), blockview(p1, None, 0), blockview(vp, 2, 1), blockview(p3, None, 0)]
 
     def stack(count):
         return jnp.concatenate([wide(v) for v in views[:count]], axis=0)
 
+    def gram_row(n, y, acc):
+        def body(a, acc):
+            p = views[n](y, a)
+            parts = []
+            for i in range(n + 1):
+                q = views[i](y, a)
+                for d in range(8):
+                    parts.append(acc[i * 8 + d] + p * (pltpu.roll(q, 8 - d, 0) if d else q))
+            return tuple(parts)
+        return lax.fori_loop(0, nb, body, acc)
+
+    def gram_zero(n):
+        return tuple(jnp.zeros((8, 128), F32) for _ in range(8 * (n + 1)))
+
+    def gram_end(acc):
+        d8 = jnp.zeros((8, 128), F32)
+        for k, part in enumerate(acc):
+            where = lane % 32 == (k // 8) * 8 + (row + k % 8) % 8
+            d8 = jnp.where(where, jnp.sum(part, axis=1, keepdims=True), d8)
+        return d8
+
     def gram(n):
-        d = dot_nt(wide(views[n]), stack(n + 1))
-        w = 8 * (n + 1)
-        rep_l = lax.broadcasted_iota(jnp.int32, (w, 128), 0)
-        rep_m = lax.broadcasted_iota(jnp.int32, (w, 128), 1)
-        return dot_nn(d, jnp.where(rep_m % 32 == rep_l, 1.0, 0.0).astype(F32))
-
-    def peer(d):
-        t = lax.rem(me + d, ndev)
-        return (t // (ny * nz), (t // nz) % ny, t % nz)
+        acc = gram_zero(n)
+        for y in range(ly):
+            acc = gram_row(n, y, acc)
+        return gram_end(acc)
 
     def ar_start(m, d8):
         packed = jnp.where(lane // 32 == row % 4, d8, 0.0)
@@ -230,29 +262,6 @@
                 return acc + ce[5 + side, y, j].reshape(nb, 8, 128) * xb[n, side, y, at, :][None]
             acc = lax.fori_loop(0, nb, body, acc)
         return acc.reshape(nb * 8, 128)
-
-    for y in order:
-        vp[1, 1 + y] = x_terms(0, y, local_terms(0, y))
-        send_row(1, y)
-    red0 = ar_done(0)
-    sigma = jnp.broadcast_to(red0[0:1, 8:9] / (8.0 * cells), (8, 128))
-    nu = jnp.broadcast_to(red0[0:1, 9:10] / (8.0 * cells), (8, 128))
-    inv = 1.0 / nu
-    sig1, inv1 = sigma[0:1], inv[0:1]
-    for y in range(ly):
-        p1[y] = (vp[1, 1 + y] - sig1 * vp[0, 1 + y]) * inv1
-    ar_start(1, gram(1))
-
-    for y in order:
-        image = x_terms(1, y, local_terms(1, y))
-        vp[2, 1 + y] = ((image - sig1 * vp[1, 1 + y]) * inv1 - sig1 * p1[y]) * inv1
-        send_row(2, y)
-    ar_start(2, gram(2))
-
-    for y in order:
-        image = x_terms(2, y, local_terms(2, y))
-        p3[y] = (image - sig1 * vp[2, 1 + y]) * inv1
-    ar_start(3, gram(3))
 
     weights, factors = [], []
     empty = jnp.zeros((8, 128), F32)
@@ -296,8 +305,35 @@
                 ob[n, pl.ds(a * nr * ly + y, 8, stride=ly), :] = q[:, c:c + 128]
         pltpu.make_async_copy(ob.at[n], basis_hbm.at[n], out_sem.at[n]).start()
 
+    for y in order:
+        vp[1, 1 + y] = x_terms(0, y, local_terms(0, y))
+        send_row(1, y)
+    red0 = ar_done(0)
+    sigma = jnp.broadcast_to(red0[0:1, 8:9] / (8.0 * cells), (8, 128))
+    nu = jnp.broadcast_to(red0[0:1, 9:10] / (8.0 * cells), (8, 128))
+    inv = 1.0 / nu
+    sig1, inv1 = sigma[0:1], inv[0:1]
+    for y in range(ly):
+        p1[y] = (vp[1, 1 + y] - sig1 * vp[0, 1 + y]) * inv1
+    ar_start(1, gram(1))
     factor(0, red0)
     emit(0)
+
+    acc = gram_zero(2)
+    for y in order:
+        image = x_terms(1, y, local_terms(1, y))
+        vp[2, 1 + y] = ((image - sig1 * vp[1, 1 + y]) * inv1 - sig1 * p1[y]) * inv1
+        send_row(2, y)
+        acc = gram_row(2, y, acc)
+    ar_start(2, gram_end(acc))
+
+    acc = gram_zero(3)
+    for y in order:
+        image = x_terms(2, y, local_terms(2, y))
+        p3[y] = (image - sig1 * vp[2, 1 + y]) * inv1
+        acc = gram_row(3, y, acc)
+    ar_start(3, gram_end(acc))
+
     factor(1, ar_done(1))
     emit(1)
     factor(2, ar_done(2))
@@ -359,7 +395,7 @@
             dma((ITERS + 1,)), dma((ITERS + 1,)),
             dma((2,)), dma((ITERS + 1,)),
         ],
-        compiler_params=pltpu.CompilerParams(has_side_effects=True, vmem_limit_bytes=48 * 1024 * 1024),
+        compiler_params=pltpu.CompilerParams(collective_id=0, has_side_effects=True, vmem_limit_bytes=48 * 1024 * 1024),
     )(rhs2, blk2)
     basis = basis.reshape(ITERS + 1, nb, nr, lx, ly, lz)
     hess = hess[:24, :32].reshape(3, 8, 4, 8).transpose(2, 3, 0, 1)

time: 36.5 us -> 34 us (0.932)
  Pallas kernels: 32.1 us -> 29.6 us
    pallas_call x1, Pallas kernels: 32.1 us -> 29.6 us  [shards(): pl.pallas_call(functools.partial(kernel, mesh_sizes, nb, nr, ly, lz), out...]
where the time goes in v2:
time: 34 us; the launch traced here: 33.8 us
  Pallas kernels  29.6 us (87%)
  local copies, waits for them, and re-layouts  3.5 us (10%)
  between operations  0.66 us (2%)
    pallas_call x1, Pallas kernels, shards(): pl.pallas_call(functools.partial(kernel, mesh_sizes, nb, nr, ly, lz), out...  29.6 us
    unnamed x5, local copies, waits for them, and re-layouts  2.71 us
    reshape x2, local copies, waits for them, and re-layouts, shards(): hess = hess[:24, :32].reshape(3, 8, 4, 8).transpose(2, 3, 0, 1)  0.79 us

profile of v2, /device:TPU:0, one launch (start us, length us, event | category | flops | bytes accessed | tf_op | source)
XLA Modules:
  0.0 33.8 jit_solution(14158888055322409826)
XLA Ops:
  0.6 0.0 copy-start
  0.6 1.0 %copy-done = bf16[7,8,8,1,4,128]{5,4,3,2,1,0:T(4,128)(2,1)S(1)} copy-done((bf16[7,8,8,1,4,128]{5,4,3,2,1,0:T(4,128)(2,1)S(1)}, bf16[7,8,8,1,4,128]{5,4,3,2,1,0:T(4,128)(2,1)}, u32[]{:S(2)}) %copy-start) | copy-done | bytes 458776
  1.6 0.0 copy-start.1
  1.7 0.9 %copy-done.1 = f32[8,8,1,4,128]{4,3,2,1,0:T(4,128)S(1)} copy-done((f32[8,8,1,4,128]{4,3,2,1,0:T(4,128)S(1)}, f32[8,8,1,4,128]{4,3,2,1,0:T(4,128)}, u32[]{:S(2)}) %copy-start.1) | copy-done | bytes 131096
  2.6 29.6 %shard_map.41 = (f32[4,256,128]{2,1,0:T(8,128)S(1)}, f32[32,128]{1,0:T(8,128)S(1)}) custom-call(f32[256,128]{1,0:T(8,128)S(1)} %bitcast.8, bf16[7,8,32,128]{3,2,1,0:T(8,128)(2,1)S(1)} %bitcast.7), custom_call_target="tpu_custom_call" | custom-call | tf_op jit(solution)/shard_map/pallas_call | solution.py:371
  32.2 0.1 reshape.19
  32.3 0.7 %copy.4 = f32[3,8,4,8]{1,3,0,2:T(8,128)} copy(f32[3,8,4,8]{3,2,1,0:T(4,128)S(1)} %reshape.19) | data formatting | bytes 6144 | tf_op jit(solution)/shard_map/reshape | solution.py:401
  33.0 0.8 %copy.7 = f32[4,8,8,1,4,128]{5,4,3,2,1,0:T(4,128)} copy(f32[4,8,8,1,4,128]{5,4,3,2,1,0:T(4,128)S(1)} %bitcast.6) | data formatting | bytes 1048576
  (1 shorter events, 0.0 us)
Async XLA Ops:
  0.6 1.0 %copy-start = (bf16[7,8,8,1,4,128]{5,4,3,2,1,0:T(4,128)(2,1)S(1)}, bf16[7,8,8,1,4,128]{5,4,3,2,1,0:T(4,128)(2,1)}, u32[]{:S(2)}) copy-start(bf16[7,8,8,1,4,128]{5,4,3,2,1,0:T(4,128)(2,1)} %param.3) | copy-start | bytes 1376260
  1.6 0.9 %copy-start.1 = (f32[8,8,1,4,128]{4,3,2,1,0:T(4,128)S(1)}, f32[8,8,1,4,128]{4,3,2,1,0:T(4,128)}, u32[]{:S(2)}) copy-start(f32[8,8,1,4,128]{4,3,2,1,0:T(4,128)} %param.2) | copy-start | bytes 393220

commit v3 on v2

--- a/solution.py
+++ b/solution.py
@@ -25,7 +25,7 @@
     mesh_sizes, nb, nr, ly, lz,
     rhs_hbm, blk_hbm, basis_hbm, hess_ref,
     rv, bv, vp, p1, p3, xb, zs, zr, ce, zp, ab, ob,
-    x_send, x_recv, y_send, y_recv, z_send, z_recv, a_send, a_recv, in_sem, out_sem,
+    x_send, x_recv, y_send, y_recv, z_send, z_recv, a_send, a_recv, in_sem, out_sem, known,
 ):
     nx, ny, nz = mesh_sizes
     ndev = nx * ny * nz
@@ -42,15 +42,21 @@
 
     barrier = pltpu.get_barrier_semaphore()
 
-    def greet(d, c):
-        pl.semaphore_signal(barrier, inc=1, device_id=peer(d), device_id_type=pl.DeviceIdType.MESH)
-        return c
+    def greet(sem, axis):
+        size, at = {"gx": (nx, gx), "gy": (ny, gy), "gz": (nz, gz)}[axis]
+
+        def body(d, c):
+            pl.semaphore_signal(sem, inc=1, device_id={axis: lax.rem(at + d, size)},
+                                device_id_type=pl.DeviceIdType.MESH)
+            return c
+        lax.fori_loop(1, size, body, 0)
 
     in_rhs = pltpu.make_async_copy(rhs_hbm, rv, in_sem.at[0])
     in_blk = pltpu.make_async_copy(blk_hbm, bv, in_sem.at[1])
     in_rhs.start()
     in_blk.start()
-    lax.fori_loop(1, ndev, greet, 0)
+    for axis in AXES:
+        greet(barrier, axis)
 
     if nx == 1:
         x_sides = []
@@ -137,9 +143,12 @@
     for y in order:
         for a in range(nb):
             vp[0, 1 + y, a * 8:(a + 1) * 8] = rv[pl.ds(a * nr * ly + y, 8, stride=ly), :]
-    pl.semaphore_wait(barrier, ndev - 1)
+    pl.semaphore_wait(barrier, nx + ny + nz - 3)
+    greet(known.at[0], "gy")
     for y in order:
         send_row(0, y)
+    pl.semaphore_wait(known.at[0], ny - 1)
+    greet(known.at[1], "gx")
 
     in_blk.wait()
     terms = [0, 3, 4, 5, 6] + [e[0] for e in x_sides]
@@ -227,6 +236,7 @@
     d0 = gram(0)
     d0 = d0 + jnp.where(lane % 32 == 8, lane_sum(trace), 0.0)
     d0 = d0 + jnp.where(lane % 32 == 9, lane_sum(total_abs), 0.0)
+    pl.semaphore_wait(known.at[1], nx - 1)
     ar_start(0, d0)
 
     def local_terms(n, y):
@@ -316,8 +326,6 @@
     for y in range(ly):
         p1[y] = (vp[1, 1 + y] - sig1 * vp[0, 1 + y]) * inv1
     ar_start(1, gram(1))
-    factor(0, red0)
-    emit(0)
 
     acc = gram_zero(2)
     for y in order:
@@ -333,6 +341,8 @@
         p3[y] = (image - sig1 * vp[2, 1 + y]) * inv1
         acc = gram_row(3, y, acc)
     ar_start(3, gram_end(acc))
+    factor(0, red0)
+    emit(0)
 
     factor(1, ar_done(1))
     emit(1)
@@ -394,6 +404,7 @@
             dma((ITERS, 2, ly)), dma((ITERS, 2, ly)),
             dma((ITERS + 1,)), dma((ITERS + 1,)),
             dma((2,)), dma((ITERS + 1,)),
+            pltpu.SemaphoreType.REGULAR((2,)),
         ],
         compiler_params=pltpu.CompilerParams(collective_id=0, has_side_effects=True, vmem_limit_bytes=48 * 1024 * 1024),
     )(rhs2, blk2)

time: 34 us -> 33 us (0.971)
  Pallas kernels: 29.6 us -> 28.7 us
    pallas_call x1, Pallas kernels: 29.6 us -> 28.7 us  [shards(): pl.pallas_call(functools.partial(kernel, mesh_sizes, nb, nr, ly, lz), out...]
where the time goes in v3:
time: 33 us; the launch traced here: 32.8 us
  Pallas kernels  28.7 us (87%)
  local copies, waits for them, and re-layouts  3.5 us (11%)
  between operations  0.66 us (2%)
    pallas_call x1, Pallas kernels, shards(): pl.pallas_call(functools.partial(kernel, mesh_sizes, nb, nr, ly, lz), out...  28.7 us
    unnamed x5, local copies, waits for them, and re-layouts  2.71 us
    reshape x2, local copies, waits for them, and re-layouts, shards(): hess = hess[:24, :32].reshape(3, 8, 4, 8).transpose(2, 3, 0, 1)  0.79 us

profile of v3, /device:TPU:0, one launch (start us, length us, event | category | flops | bytes accessed | tf_op | source)
XLA Modules:
  0.0 32.8 jit_solution(9028067164519100724)
XLA Ops:
  0.6 0.0 copy-start
  0.6 1.0 %copy-done = bf16[7,8,8,1,4,128]{5,4,3,2,1,0:T(4,128)(2,1)S(1)} copy-done((bf16[7,8,8,1,4,128]{5,4,3,2,1,0:T(4,128)(2,1)S(1)}, bf16[7,8,8,1,4,128]{5,4,3,2,1,0:T(4,128)(2,1)}, u32[]{:S(2)}) %copy-start) | copy-done | bytes 458776
  1.6 0.0 copy-start.1
  1.7 0.9 %copy-done.1 = f32[8,8,1,4,128]{4,3,2,1,0:T(4,128)S(1)} copy-done((f32[8,8,1,4,128]{4,3,2,1,0:T(4,128)S(1)}, f32[8,8,1,4,128]{4,3,2,1,0:T(4,128)}, u32[]{:S(2)}) %copy-start.1) | copy-done | bytes 131096
  2.6 28.7 %shard_map.41 = (f32[4,256,128]{2,1,0:T(8,128)S(1)}, f32[32,128]{1,0:T(8,128)S(1)}) custom-call(f32[256,128]{1,0:T(8,128)S(1)} %bitcast.8, bf16[7,8,32,128]{3,2,1,0:T(8,128)(2,1)S(1)} %bitcast.7), custom_call_target="tpu_custom_call" | custom-call | tf_op jit(solution)/shard_map/pallas_call | solution.py:381
  31.2 0.1 reshape.19
  31.3 0.7 %copy.4 = f32[3,8,4,8]{1,3,0,2:T(8,128)} copy(f32[3,8,4,8]{3,2,1,0:T(4,128)S(1)} %reshape.19) | data formatting | bytes 6144 | tf_op jit(solution)/shard_map/reshape | solution.py:412
  32.0 0.8 %copy.7 = f32[4,8,8,1,4,128]{5,4,3,2,1,0:T(4,128)} copy(f32[4,8,8,1,4,128]{5,4,3,2,1,0:T(4,128)S(1)} %bitcast.6) | data formatting | bytes 1048576
  (1 shorter events, 0.0 us)
Async XLA Ops:
  0.6 1.0 %copy-start = (bf16[7,8,8,1,4,128]{5,4,3,2,1,0:T(4,128)(2,1)S(1)}, bf16[7,8,8,1,4,128]{5,4,3,2,1,0:T(4,128)(2,1)}, u32[]{:S(2)}) copy-start(bf16[7,8,8,1,4,128]{5,4,3,2,1,0:T(4,128)(2,1)} %param.3) | copy-start | bytes 1376260
  1.6 0.9 %copy-start.1 = (f32[8,8,1,4,128]{4,3,2,1,0:T(4,128)S(1)}, f32[8,8,1,4,128]{4,3,2,1,0:T(4,128)}, u32[]{:S(2)}) copy-start(f32[8,8,1,4,128]{4,3,2,1,0:T(4,128)} %param.2) | copy-start | bytes 393220
